TPU v7x, 32 devices: a whole 2x2x4 slice. The times are simulated.
32 devices in a mesh: groups: 2 (over x), blk: 16 (over z, y, core).
Axes of the slice: x: 2, y: 2, z: 4, core: 2. Of those that a mesh axis runs over, the one named last changes fastest.
Arguments:
- embeddings: bfloat16 [12288, 512], P(('groups', 'blk')), parts along dimension 0, may hold values from -24 to 24
- cluster_ids: int32 [12288], P(('groups', 'blk')), parts along dimension 0, may hold values from 0 to 63, as said below
- cluster_sizes: int32 [128], P('groups'), parts along dimension 0, may hold values from 12 to 960, as said below
Outputs:
- log_density: float32 [12288], P(('groups', 'blk')), parts along dimension 0
- centrality: float32 [12288], P(('groups', 'blk')), parts along dimension 0
There are 2 independent parts, one for each index of `groups`. A program takes and returns all parts, laid end to end along the dimension named above; each array names one. Nothing has to cross between parts.
Inputs may be any that keep to these rules, and one draw needn't show every extreme that they name: cluster_sizes[c] is the number of rows whose cluster id is c; the sizes sum to 6144 and the largest is exactly 960. `cluster_ids`: rows are dealt to the devices of blk: with n the number of devices of blk and E_c the sum of cluster_sizes[c'] mod n over the clusters c' < c, device s holds cluster_sizes[c] // n rows of cluster c, plus one more exactly when (s - E_c) mod n < cluster_sizes[c] mod n. Within a device the rows stand in no particular order.
All inputs are finite; a program needn't handle non-finite values.
Results may differ from a plain program's by a relative error of at most 0.00065.
The roundings to bfloat16 on the way count: a program that leaves them out, or rounds other values in their place, can miss the bound.
Values may be sent and summed in bfloat16 or wider, within the bound.
No kernel may reach another device: no remote copies, remote signals or barrier semaphores. Data moves between devices by JAX's collectives and lax.ppermute only.
A program may use at most 64 MiB of HBM per device.

v0:
```python
import jax
import jax.numpy as jnp
from jax import lax
from jax.sharding import PartitionSpec as P

SOFTMAX_TEMP = 0.1
EPSILON = 1e-06


def shifted(array, axis, by):
    peers = lax.axis_size(axis)
    pairs = [(i, i + by) for i in range(peers) if 0 <= i + by < peers]
    return lax.ppermute(array, axis, pairs)


def unit_rows(embeddings):
    values = embeddings.astype(jnp.float32)
    scale = lax.rsqrt(jnp.mean(values * values, axis=1, keepdims=True) + EPSILON)
    return (values * (scale * values.shape[1] ** (-0.5))).astype(jnp.bfloat16)


def block_terms(remaining_rows, left_labels, right_rows, right_labels):
    similarity_scores = jnp.einsum(
        "rd,kd->rk", remaining_rows, right_rows, preferred_element_type=jnp.float32
    )
    same_cluster = left_labels[:, None] == right_labels[None, :]
    return jnp.sum(jnp.where(same_cluster, jnp.exp(similarity_scores / SOFTMAX_TEMP), 0.0), axis=1)


def lookup(table, one_hot):
    return jnp.sum(jnp.where(one_hot, table[None, :], 0), axis=1)


def sorted_density(unit, cluster_sizes, member):
    devices = lax.axis_size("blk")
    own_index = lax.axis_index("blk")
    rows_dev = unit.shape[0]
    clusters = cluster_sizes.shape[0]
    total_rows = rows_dev * devices
    fewest = total_rows // 512
    largest = total_rows * 5 // 32
    capacity = min(rows_dev, rows_dev // devices + rows_dev // fewest + 2)
    reach = (largest + rows_dev - 2) // rows_dev
    ends = jnp.cumsum(cluster_sizes)
    starts = ends - cluster_sizes
    base = cluster_sizes // devices
    extra = cluster_sizes % devices
    first = (jnp.cumsum(extra) - extra) % devices
    source_rows = jnp.arange(devices, dtype=jnp.int32)
    holds = base[None, :] + (
        (source_rows[:, None] - first[None, :]) % devices < extra[None, :]
    ).astype(jnp.int32)
    member_count = jnp.cumsum(member.astype(jnp.int32), axis=0)
    rank = jnp.sum(jnp.where(member, member_count - 1, 0), axis=1)
    held_row = jnp.dot(
        member.astype(jnp.float32), holds.T.astype(jnp.float32), precision=lax.Precision.HIGHEST
    ).astype(jnp.int32)
    before_me = (source_rows[None, :] < own_index) & (held_row > rank[:, None])
    within = jnp.sum(jnp.minimum(held_row, rank[:, None]), axis=1) + jnp.sum(
        before_me.astype(jnp.int32), axis=1
    )
    position = lookup(starts, member) + within
    target = position // rows_dev
    earlier = (target[None, :] == target[:, None]) & (position[None, :] < position[:, None])
    slot = jnp.sum(earlier.astype(jnp.int32), axis=1)
    address = target * capacity + slot
    sender = (
        jnp.zeros((devices * capacity,), jnp.int32)
        .at[address]
        .set(jnp.arange(rows_dev, dtype=jnp.int32))
    )
    filled = jnp.zeros((devices * capacity,), jnp.bool_).at[address].set(True)
    packed = jnp.where(filled[:, None], unit[sender], jnp.zeros((), jnp.bfloat16))
    arrived = lax.all_to_all(packed, "blk", split_axis=0, concat_axis=0, tiled=True)
    local = jnp.arange(rows_dev, dtype=jnp.int32)
    places = own_index * rows_dev + local
    home_label = jnp.sum((places[:, None] >= ends[None, :]).astype(jnp.int32), axis=1)
    home_cluster_member = home_label[:, None] == jnp.arange(clusters, dtype=jnp.int32)[None, :]
    offset_in = places - lookup(starts, home_cluster_member)
    base_row = lookup(base, home_cluster_member)
    extra_row = lookup(extra, home_cluster_member)
    first_row = lookup(first, home_cluster_member)
    full_rounds = devices * base_row
    surplus = offset_in - full_rounds
    wrapped = first_row + extra_row - devices
    late_source = jnp.where(
        wrapped > 0,
        jnp.where(surplus < wrapped, surplus, first_row + surplus - wrapped),
        first_row + surplus,
    )
    anchor = jnp.where(offset_in < full_rounds, offset_in % devices, late_source)
    anchor_hot = anchor[:, None] == source_rows[None, :]
    anchor_count = jnp.cumsum(anchor_hot.astype(jnp.int32), axis=0)
    order_in = jnp.sum(jnp.where(anchor_hot, anchor_count - 1, 0), axis=1)
    block = arrived[anchor * capacity + order_in]

    def labels_at(spots):
        inside = (spots >= 0) & (spots < total_rows)
        found = jnp.sum((spots[:, None] >= ends[None, :]).astype(jnp.int32), axis=1)
        return jnp.where(inside, found, -1)

    density = block_terms(block, home_label, block, home_label)

    def advance(offset, carried_rows):
        upper, lower, running = carried_rows
        upper = shifted(upper, "blk", 1)
        lower = shifted(lower, "blk", -1)
        running = running + block_terms(
            block, home_label, upper, labels_at(places - offset * rows_dev)
        )
        running = running + block_terms(
            block, home_label, lower, labels_at(places + offset * rows_dev)
        )
        return (upper, lower, running)

    carried_out = lax.fori_loop(1, reach + 1, advance, (block, block, density))
    density = carried_out[2]
    returned = (
        jnp.zeros((devices * capacity,), jnp.float32).at[anchor * capacity + order_in].set(density)
    )
    answered = lax.all_to_all(returned, "blk", split_axis=0, concat_axis=0, tiled=True)
    return answered[address]


def on_device(embeddings, cluster_ids, cluster_sizes):
    unit = unit_rows(embeddings)
    clusters = cluster_sizes.shape[0]
    member = cluster_ids[:, None] == jnp.arange(clusters, dtype=jnp.int32)[None, :]
    partial_sum = jnp.einsum(
        "rc,rd->cd", member.astype(jnp.bfloat16), unit, preferred_element_type=jnp.float32
    )
    centroid = lax.psum(partial_sum, "blk")
    density = sorted_density(unit, cluster_sizes, member)
    sizes_row = lookup(cluster_sizes, member).astype(jnp.float32)
    log_density = jnp.log(density / sizes_row)
    projected = jnp.dot(unit.astype(jnp.float32), centroid.T, precision=lax.Precision.HIGHEST)
    centrality = jnp.sum(jnp.where(member, projected, 0.0), axis=1) / sizes_row
    return (log_density, centrality)


def solution(mesh):
    in_specs = (P(("groups", "blk"), None), P(("groups", "blk")), P("groups"))
    out_specs = (P(("groups", "blk")), P(("groups", "blk")))
    return jax.shard_map(
        on_device, mesh=mesh, in_specs=in_specs, out_specs=out_specs, check_vma=False
    )
```

profile of v0, /device:TPU:8, one launch (start us, length us, event | category | flops | bytes accessed | tf_op | source)
XLA Modules:
  0.0 142.4 jit_solution(12733876175211087510)
XLA Ops:
  7.2 1.2 fusion.14
  8.4 0.1 fusion.15
  8.6 0.0 copy-start.2
  8.6 0.6 copy-done.2
  9.2 0.1 copy.17
  9.3 0.1 reduce-window.37
  9.4 0.1 reduce
  9.5 0.1 copy.18
  9.6 0.1 reduce-window.38
  9.7 0.1 reduce.1
  9.9 0.0 copy-start.1
  9.9 0.1 convert_reduce_fusion.3
  10.0 0.6 copy-done.1
  10.6 0.9 reduce-window.41
  11.5 0.2 slice_reduce_fusion
  11.7 0.2 select_reduce_fusion
  11.9 0.3 convert_reduce_fusion.4
  12.3 0.3 convert_reduce_fusion.2
  12.6 2.9 %scatter_custom_fusion.1 = s32[928]{0:T(1024)S(1)} fusion(s32[384]{0:T(512)S(1)} %fusion.58, s32[384]{0:T(512)S(1)} %iota.57, s32[]{:T(128)} %copy.40), kind=kCustom, calls=%fused_computation.120 | custom fusion | bytes 3716 | tf_op jit(solution)/shard_map/scatter | solution.py:70
  15.5 4.0 %gather_fusion = bf16[928,512]{1,0:T(8,128)(2,1)S(1)} fusion(bf16[384,512]{1,0:T(8,128)(2,1)S(1)} %fusion.15, s32[1024]{0:T(1024)S(1)} %pad_clamp_fusion.2), kind=kCustom, calls=%fused_computation | custom fusion | bytes 1904256 | tf_op jit(solution)/shard_map/gather | solution.py:73
  19.6 0.2 gather.12
  19.8 2.0 %scatter_custom_fusion = pred[928]{0:T(1024)(128)(4,1)S(1)} fusion(s32[384]{0:T(512)S(1)} %fusion.58, pred[384]{0:T(512)(128)(4,1)S(1)} %broadcast.470, pred[]{:T(512)} %constant.152.clone.1), kind=kCustom, calls=%fused_computation.132 | custom fusion | bytes 929 | tf_op jit(solution)/shard_map/scatter | solution.py:72
  21.8 0.1 broadcast_in_dim.158
  21.9 1.2 broadcast_select_fusion
  23.1 6.3 %all-to-all-start = ((bf16[16,58,512]{2,1,0:T(8,128)(2,1)}), bf16[16,58,512]{2,1,0:T(8,128)(2,1)S(1)}, u32[]{:S(2)}, u32[]{:S(2)}) async-start(bf16[16,58,512]{2,1,0:T(8,128)(2,1)} %broadcast_select_fusion), calls=%async_computation | async-start | bytes 2097152 | tf_op jit(solution)/shard_map/all_to_all | solution.py:74
  29.4 0.0 all-reduce.2.cloned.1.call-start
  29.5 0.8 fusion.18
  30.3 0.0 all-reduce.2.cloned.1.call-update
  30.4 0.9 reduce-window.39
  31.2 0.2 slice_reduce_fusion.1
  31.5 0.1 fusion.34
  31.7 22.5 %all-to-all-done = bf16[16,58,512]{2,1,0:T(8,128)(2,1)S(1)} async-done(((bf16[16,58,512]{2,1,0:T(8,128)(2,1)}), bf16[16,58,512]{2,1,0:T(8,128)(2,1)S(1)}, u32[]{:S(2)}, u32[]{:S(2)}) %all-to-all-start) | async-done | bytes 950304 | tf_op jit(solution)/shard_map/all_to_all | solution.py:74
  54.2 0.3 all_to_all.15
  54.4 2.1 %gather_fusion.1 = bf16[384,512]{1,0:T(8,128)(2,1)S(1)} fusion(bf16[928,512]{1,0:T(8,128)(2,1)S(1)} %all_to_all.15, s32[1024]{0:T(1024)S(1)} %pad_clamp_fusion.1), kind=kCustom, calls=%fused_computation.1 | custom fusion | bytes 787968 | tf_op jit(solution)/shard_map/gather | solution.py:95
  56.6 0.4 fusion.12
  57.0 38.6 %while.18 = (s32[]{:T(128)}, bf16[384,512]{1,0:T(8,128)(2,1)S(1)}, bf16[384,512]{1,0:T(8,128)(2,1)S(1)}, f32[384]{0:T(512)S(1)}, s32[384]{0:T(512)S(1)}, /*index...) while((s32[]{:T(128)}, bf16[384,512]{1,0:T(8,128)(2,1)S(1)}, ...), condition=%wide.region_26.27_spmd.clone, body=%wide.region_21.26_spmd.clone.sunk | while | flops 303321984 | bytes 6322649 | solution.py:116
  57.0 2.9 %collective-permute-start = (bf16[384,512]{1,0:T(8,128)(2,1)S(1)}, bf16[384,512]{1,0:T(8,128)(2,1)S(1)}, u32[]{:S(2)}, u32[]{:S(2)}) collective-permute-start(bf16[384,512]{1,0:T(8,128)(2,1)S(1)} %get-tuple-element.275), channel_id=1, source_target_pairs={{0,1},{1,2},{2,3},{3,4},{4,5},{5,6},{6,7},{7,8},{8,9},{9,10},{10,1... | collective-permute-start | bytes 1179656 | tf_op jit(solution)/shard_map/while/body/eval_jaxpr/ppermute | solution.py:13
  59.9 3.5 %collective-permute-start.1 = (bf16[384,512]{1,0:T(8,128)(2,1)S(1)}, bf16[384,512]{1,0:T(8,128)(2,1)S(1)}, u32[]{:S(2)}, u32[]{:S(2)}) collective-permute-start(bf16[384,512]{1,0:T(8,128)(2,1)S(1)} %get-tuple-element.276), channel_id=1, source_target_pairs={{1,0},{2,1},{3,2},{4,3},{5,4},{6,5},{7,6},{8,7},{9,8},{10,9},{11,1... | collective-permute-start | bytes 1179656 | tf_op jit(solution)/shard_map/while/body/eval_jaxpr/ppermute | solution.py:13
  63.5 0.1 convert_reduce_fusion.6
  63.6 5.1 %collective-permute-done.1 = bf16[384,512]{1,0:T(8,128)(2,1)S(1)} collective-permute-done((bf16[384,512]{1,0:T(8,128)(2,1)S(1)}, bf16[384,512]{1,0:T(8,128)(2,1)S(1)}, u32[]{:S(2)}, u32[]{:S(2)}) %collective-permute-start.1) | collective-permute-done | bytes 393248 | tf_op jit(solution)/shard_map/while/body/eval_jaxpr/ppermute | solution.py:13
  68.7 0.4 fusion.89
  69.2 0.4 fusion.90
  69.7 4.3 %collective-permute-start = (bf16[384,512]{1,0:T(8,128)(2,1)S(1)}, bf16[384,512]{1,0:T(8,128)(2,1)S(1)}, u32[]{:S(2)}, u32[]{:S(2)}) collective-permute-start(bf16[384,512]{1,0:T(8,128)(2,1)S(1)} %get-tuple-element.275), channel_id=1, source_target_pairs={{0,1},{1,2},{2,3},{3,4},{4,5},{5,6},{6,7},{7,8},{8,9},{9,10},{10,1... | collective-permute-start | bytes 1179656 | tf_op jit(solution)/shard_map/while/body/eval_jaxpr/ppermute | solution.py:13
  74.0 2.3 %collective-permute-start.1 = (bf16[384,512]{1,0:T(8,128)(2,1)S(1)}, bf16[384,512]{1,0:T(8,128)(2,1)S(1)}, u32[]{:S(2)}, u32[]{:S(2)}) collective-permute-start(bf16[384,512]{1,0:T(8,128)(2,1)S(1)} %get-tuple-element.276), channel_id=1, source_target_pairs={{1,0},{2,1},{3,2},{4,3},{5,4},{6,5},{7,6},{8,7},{9,8},{10,9},{11,1... | collective-permute-start | bytes 1179656 | tf_op jit(solution)/shard_map/while/body/eval_jaxpr/ppermute | solution.py:13
  76.3 0.1 convert_reduce_fusion.6
  76.5 5.2 %collective-permute-done.1 = bf16[384,512]{1,0:T(8,128)(2,1)S(1)} collective-permute-done((bf16[384,512]{1,0:T(8,128)(2,1)S(1)}, bf16[384,512]{1,0:T(8,128)(2,1)S(1)}, u32[]{:S(2)}, u32[]{:S(2)}) %collective-permute-start.1) | collective-permute-done | bytes 393248 | tf_op jit(solution)/shard_map/while/body/eval_jaxpr/ppermute | solution.py:13
  81.7 0.4 fusion.89
  82.1 0.4 fusion.90
  82.6 4.2 %collective-permute-start = (bf16[384,512]{1,0:T(8,128)(2,1)S(1)}, bf16[384,512]{1,0:T(8,128)(2,1)S(1)}, u32[]{:S(2)}, u32[]{:S(2)}) collective-permute-start(bf16[384,512]{1,0:T(8,128)(2,1)S(1)} %get-tuple-element.275), channel_id=1, source_target_pairs={{0,1},{1,2},{2,3},{3,4},{4,5},{5,6},{6,7},{7,8},{8,9},{9,10},{10,1... | collective-permute-start | bytes 1179656 | tf_op jit(solution)/shard_map/while/body/eval_jaxpr/ppermute | solution.py:13
  86.8 2.4 %collective-permute-start.1 = (bf16[384,512]{1,0:T(8,128)(2,1)S(1)}, bf16[384,512]{1,0:T(8,128)(2,1)S(1)}, u32[]{:S(2)}, u32[]{:S(2)}) collective-permute-start(bf16[384,512]{1,0:T(8,128)(2,1)S(1)} %get-tuple-element.276), channel_id=1, source_target_pairs={{1,0},{2,1},{3,2},{4,3},{5,4},{6,5},{7,6},{8,7},{9,8},{10,9},{11,1... | collective-permute-start | bytes 1179656 | tf_op jit(solution)/shard_map/while/body/eval_jaxpr/ppermute | solution.py:13
  89.3 0.1 convert_reduce_fusion.6
  89.4 5.2 %collective-permute-done.1 = bf16[384,512]{1,0:T(8,128)(2,1)S(1)} collective-permute-done((bf16[384,512]{1,0:T(8,128)(2,1)S(1)}, bf16[384,512]{1,0:T(8,128)(2,1)S(1)}, u32[]{:S(2)}, u32[]{:S(2)}) %collective-permute-start.1) | collective-permute-done | bytes 393248 | tf_op jit(solution)/shard_map/while/body/eval_jaxpr/ppermute | solution.py:13
  94.6 0.4 fusion.89
  95.0 0.4 fusion.90
  95.5 2.9 %scatter_custom_fusion.2 = f32[928]{0:T(1024)S(1)} fusion(s32[384]{0:T(512)S(1)} %fusion.57, f32[384]{0:T(512)S(1)} %get-tuple-element.141, f32[]{:T(128)} %constant.139.clone.1), kind=kCustom, calls=%fused_computation.128 | custom fusion | bytes 3716 | tf_op jit(solution)/shard_map/scatter | solution.py:119
  98.5 0.7 all_to_all.16
  99.1 8.8 %all-to-all-start.1 = ((f32[16,58,1]{1,2,0:T(1,128)}), f32[16,58,1]{1,2,0:T(1,128)S(1)}, u32[]{:S(2)}, u32[]{:S(2)}) async-start(f32[16,58,1]{1,2,0:T(1,128)} %bitcast.9), calls=%async_computation.1 | async-start | bytes 16384 | tf_op jit(solution)/shard_map/all_to_all | solution.py:121
  107.9 22.5 %all-reduce.2.cloned.1.call-done = f32[64,512]{1,0:T(8,128)} async-done(((f32[64,512]{1,0:T(8,128)}), f32[64,512]{1,0:T(8,128)}) %all-reduce.2.cloned.1.call-update) | async-done | bytes 131088 | tf_op jit(solution)/shard_map/psum | solution.py:132
  130.4 1.4 fusion.13
  131.8 0.5 broadcast.549
  132.3 0.7 reduce.13
  133.0 0.1 all_to_all.18
  133.0 1.9 %gather_fusion.2 = f32[384]{0:T(512)S(1)} fusion(f32[928]{0:T(1024)S(1)} %all_to_all.18, s32[1024]{0:T(1024)S(1)} %pad_clamp_fusion), kind=kCustom, calls=%fused_computation.2 | custom fusion | bytes 4608 | tf_op jit(solution)/shard_map/gather | solution.py:122
  134.9 0.6 convert_divide_fusion
  (46 shorter events, 0.6 us)
Async XLA Ops:
  7.2 1.2 copy-start
  8.6 0.7 copy-start.2
  9.9 0.7 copy-start.1
  23.1 31.0 %all-to-all-start = ((bf16[16,58,512]{2,1,0:T(8,128)(2,1)}), bf16[16,58,512]{2,1,0:T(8,128)(2,1)S(1)}, u32[]{:S(2)}, u32[]{:S(2)}) async-start(bf16[16,58,512]{2,1,0:T(8,128)(2,1)} %broadcast_select_fusion), calls=%async_computation | async-start | bytes 2097152 | tf_op jit(solution)/shard_map/all_to_all | solution.py:74
  29.4 101.0 %all-reduce.2.cloned.1.call-start = ((), (), s32[]{:S(2)}) async-start(), calls=%async_computation.2 | async-start | bytes 262144 | tf_op jit(solution)/shard_map/psum | solution.py:132
  57.0 12.2 %collective-permute-start = (bf16[384,512]{1,0:T(8,128)(2,1)S(1)}, bf16[384,512]{1,0:T(8,128)(2,1)S(1)}, u32[]{:S(2)}, u32[]{:S(2)}) collective-permute-start(bf16[384,512]{1,0:T(8,128)(2,1)S(1)} %get-tuple-element.275), channel_id=1, source_target_pairs={{0,1},{1,2},{2,3},{3,4},{4,5},{5,6},{6,7},{7,8},{8,9},{9,10},{10,1... | collective-permute-start | bytes 1179656 | tf_op jit(solution)/shard_map/while/body/eval_jaxpr/ppermute | solution.py:13
  59.9 8.8 %collective-permute-start.1 = (bf16[384,512]{1,0:T(8,128)(2,1)S(1)}, bf16[384,512]{1,0:T(8,128)(2,1)S(1)}, u32[]{:S(2)}, u32[]{:S(2)}) collective-permute-start(bf16[384,512]{1,0:T(8,128)(2,1)S(1)} %get-tuple-element.276), channel_id=1, source_target_pairs={{1,0},{2,1},{3,2},{4,3},{5,4},{6,5},{7,6},{8,7},{9,8},{10,9},{11,1... | collective-permute-start | bytes 1179656 | tf_op jit(solution)/shard_map/while/body/eval_jaxpr/ppermute | solution.py:13
  69.7 12.4 %collective-permute-start = (bf16[384,512]{1,0:T(8,128)(2,1)S(1)}, bf16[384,512]{1,0:T(8,128)(2,1)S(1)}, u32[]{:S(2)}, u32[]{:S(2)}) collective-permute-start(bf16[384,512]{1,0:T(8,128)(2,1)S(1)} %get-tuple-element.275), channel_id=1, source_target_pairs={{0,1},{1,2},{2,3},{3,4},{4,5},{5,6},{6,7},{7,8},{8,9},{9,10},{10,1... | collective-permute-start | bytes 1179656 | tf_op jit(solution)/shard_map/while/body/eval_jaxpr/ppermute | solution.py:13
  74.0 7.7 %collective-permute-start.1 = (bf16[384,512]{1,0:T(8,128)(2,1)S(1)}, bf16[384,512]{1,0:T(8,128)(2,1)S(1)}, u32[]{:S(2)}, u32[]{:S(2)}) collective-permute-start(bf16[384,512]{1,0:T(8,128)(2,1)S(1)} %get-tuple-element.276), channel_id=1, source_target_pairs={{1,0},{2,1},{3,2},{4,3},{5,4},{6,5},{7,6},{8,7},{9,8},{10,9},{11,1... | collective-permute-start | bytes 1179656 | tf_op jit(solution)/shard_map/while/body/eval_jaxpr/ppermute | solution.py:13
  82.6 12.4 %collective-permute-start = (bf16[384,512]{1,0:T(8,128)(2,1)S(1)}, bf16[384,512]{1,0:T(8,128)(2,1)S(1)}, u32[]{:S(2)}, u32[]{:S(2)}) collective-permute-start(bf16[384,512]{1,0:T(8,128)(2,1)S(1)} %get-tuple-element.275), channel_id=1, source_target_pairs={{0,1},{1,2},{2,3},{3,4},{4,5},{5,6},{6,7},{7,8},{8,9},{9,10},{10,1... | collective-permute-start | bytes 1179656 | tf_op jit(solution)/shard_map/while/body/eval_jaxpr/ppermute | solution.py:13
  86.8 7.7 %collective-permute-start.1 = (bf16[384,512]{1,0:T(8,128)(2,1)S(1)}, bf16[384,512]{1,0:T(8,128)(2,1)S(1)}, u32[]{:S(2)}, u32[]{:S(2)}) collective-permute-start(bf16[384,512]{1,0:T(8,128)(2,1)S(1)} %get-tuple-element.276), channel_id=1, source_target_pairs={{1,0},{2,1},{3,2},{4,3},{5,4},{6,5},{7,6},{8,7},{9,8},{10,9},{11,1... | collective-permute-start | bytes 1179656 | tf_op jit(solution)/shard_map/while/body/eval_jaxpr/ppermute | solution.py:13
  99.1 32.6 %all-to-all-start.1 = ((f32[16,58,1]{1,2,0:T(1,128)}), f32[16,58,1]{1,2,0:T(1,128)S(1)}, u32[]{:S(2)}, u32[]{:S(2)}) async-start(f32[16,58,1]{1,2,0:T(1,128)} %bitcast.9), calls=%async_computation.1 | async-start | bytes 16384 | tf_op jit(solution)/shard_map/all_to_all | solution.py:121
Sparse Core Ops, SparseCore 0:
  33.7 96.6 all-reduce.1
where the time goes:
time: 143 us; the launch traced here: 142 us
  waiting for transfers between devices  60.5 us (42%)
  starting transfers between devices  34.8 us (24%)
  local copies, waits for them, and re-layouts  19.8 us (14%)
  between operations  14.3 us (10%)
  other arithmetic  7.29 us (5%)
  matrix products  5.41 us (4%)
    all_to_all x1, waiting for transfers between devices, sorted_density(): lax.all_to_all(packed, 'blk', split_axis=0, concat_axis=0, tiled=True)  22.5 us
    psum x1, waiting for transfers between devices, on_device(): centroid = lax.psum(partial_sum, 'blk')  22.5 us
    ppermute x6, starting transfers between devices, shifted(): return lax.ppermute(array, axis, pairs)  19.7 us
    ppermute x6, waiting for transfers between devices, shifted(): return lax.ppermute(array, axis, pairs)  15.5 us
    all_to_all x1, starting transfers between devices, sorted_density(): lax.all_to_all(returned, 'blk', split_axis=0, concat_axis=0, tiled=True)  8.78 us
    all_to_all x1, starting transfers between devices, sorted_density(): lax.all_to_all(packed, 'blk', split_axis=0, concat_axis=0, tiled=True)  6.3 us
    gather x2, local copies, waits for them, and re-layouts, sorted_density(): unit[sender]  4.29 us
    scatter x1, local copies, waits for them, and re-layouts, sorted_density(): sender = jnp.zeros((devices * capacity,), jnp.int32).at[address].set(jnp....  2.92 us
  transfers between devices with their start and end apart: 9, of which 5 were waited for; matrix products, arithmetic and copies ran while one was open for 8% of the time, Pallas kernels for 0%

commit v1 on v0

--- a/solution.py
+++ b/solution.py
@@ -5,6 +5,28 @@
 
 SOFTMAX_TEMP = 0.1
 EPSILON = 1e-06
+
+
+def split_up(value, dim, length):
+    before, after = (value.shape[:dim], value.shape[dim + 1 :])
+    return jnp.moveaxis(value.reshape(*before, length, -1, *after), dim, 0)
+
+
+def in_order(blocks, dim):
+    blocks = jnp.moveaxis(blocks, 0, dim)
+    lengths = blocks.shape
+    return blocks.reshape(*lengths[:dim], lengths[dim] * lengths[dim + 1], *lengths[dim + 2 :])
+
+
+def pairwise_exchange(value, axis, split_dim, concat_dim):
+    size, index = (lax.axis_size(axis), lax.axis_index(axis))
+    tiles = split_up(value, split_dim, size)
+    outs = [tiles[index]]
+    for step in range(1, size):
+        sent = tiles[index ^ step]
+        outs.append(lax.ppermute(sent, axis, [(i, i ^ step) for i in range(size)]))
+    tiles = jnp.stack(outs)[index ^ jnp.arange(size)]
+    return in_order(tiles, concat_dim)
 
 
 def shifted(array, axis, by):
@@ -71,7 +93,7 @@
     )
     filled = jnp.zeros((devices * capacity,), jnp.bool_).at[address].set(True)
     packed = jnp.where(filled[:, None], unit[sender], jnp.zeros((), jnp.bfloat16))
-    arrived = lax.all_to_all(packed, "blk", split_axis=0, concat_axis=0, tiled=True)
+    arrived = pairwise_exchange(packed, "blk", 0, 0)
     local = jnp.arange(rows_dev, dtype=jnp.int32)
     places = own_index * rows_dev + local
     home_label = jnp.sum((places[:, None] >= ends[None, :]).astype(jnp.int32), axis=1)

time: 143 us -> 131 us (0.916)
  the two profiles are of different devices: /device:TPU:8 before, /device:TPU:0 now
where the time goes in v1:
time: 131 us
  starting transfers between devices  65.4 us (50%)
  local copies, waits for them, and re-layouts  20.6 us (16%)
  waiting for transfers between devices  18.3 us (14%)
  between operations  14.6 us (11%)
  other arithmetic  6.29 us (5%)
  matrix products  5.42 us (4%)
    ppermute x15, starting transfers between devices, pairwise_exchange(): outs.append(lax.ppermute(sent, axis, [(i, i ^ step) for i in range(size)]))  27.2 us
    ppermute x6, starting transfers between devices, shifted(): return lax.ppermute(array, axis, pairs)  24.7 us
    all_to_all x1, starting transfers between devices, sorted_density(): lax.all_to_all(returned, 'blk', split_axis=0, concat_axis=0, tiled=True)  13.4 us
    ppermute x15, waiting for transfers between devices, pairwise_exchange(): outs.append(lax.ppermute(sent, axis, [(i, i ^ step) for i in range(size)]))  6.71 us
    ppermute x6, waiting for transfers between devices, shifted(): return lax.ppermute(array, axis, pairs)  6.53 us
    all_to_all x1, waiting for transfers between devices, sorted_density(): lax.all_to_all(returned, 'blk', split_axis=0, concat_axis=0, tiled=True)  5.02 us
    gather x2, local copies, waits for them, and re-layouts, sorted_density(): unit[sender]  4.29 us
    scatter x1, local copies, waits for them, and re-layouts, sorted_density(): jnp.zeros((devices * capacity,), jnp.float32)  2.92 us
  transfers between devices with their start and end apart: 23, of which 8 were waited for; matrix products, arithmetic and copies ran while one was open for 19% of the time, Pallas kernels for 0%

profile of v1, /device:TPU:0, one launch (start us, length us, event | category | flops | bytes accessed | tf_op | source)
XLA Modules:
  0.0 130.8 jit_solution(8712553569688075447)
XLA Ops:
  7.2 1.2 fusion.14
  8.4 0.1 fusion.15
  8.6 0.5 copy-done.1
  9.1 0.8 fusion.18
  10.0 0.6 copy-done.2
  11.4 0.9 reduce-window.41
  12.3 0.2 slice_reduce_fusion
  12.6 0.2 select_reduce_fusion
  12.9 0.9 reduce-window.39
  13.8 0.2 slice_reduce_fusion.1
  14.0 0.3 convert_reduce_fusion.4
  14.4 0.3 convert_reduce_fusion.2
  14.7 2.9 %scatter_custom_fusion.1 = s32[928]{0:T(1024)S(1)} fusion(s32[384]{0:T(512)S(1)} %fusion.59, s32[384]{0:T(512)S(1)} %iota.61, s32[]{:T(128)} %copy.55), kind=kCustom, calls=%fused_computation.155 | custom fusion | bytes 3716 | tf_op jit(solution)/shard_map/scatter | solution.py:92
  17.8 4.0 %gather_fusion = bf16[928,512]{1,0:T(8,128)(2,1)S(1)} fusion(bf16[384,512]{1,0:T(8,128)(2,1)S(1)} %fusion.15, s32[1024]{0:T(1024)S(1)} %get-tuple-element.222), kind=kCustom, calls=%fused_computation | custom fusion | bytes 1904256 | tf_op jit(solution)/shard_map/gather | solution.py:95
  21.8 0.2 gather.15
  22.1 2.0 %scatter_custom_fusion = pred[928]{0:T(1024)(128)(4,1)S(1)} fusion(s32[384]{0:T(512)S(1)} %fusion.59, pred[384]{0:T(512)(128)(4,1)S(1)} %broadcast.499, pred[]{:T(512)} %constant.168.clone.1), kind=kCustom, calls=%fused_computation.167 | custom fusion | bytes 929 | tf_op jit(solution)/shard_map/scatter | solution.py:94
  24.2 0.2 broadcast_select_fusion
  24.5 0.2 dynamic-slice_bitcast_fusion
  24.6 0.6 collective-permute-start.2
  25.2 2.6 %collective-permute-start.3 = (bf16[58,512]{1,0:T(8,128)(2,1)S(1)}, bf16[58,512]{1,0:T(8,128)(2,1)S(1)}, u32[]{:S(2)}, u32[]{:S(2)}) collective-permute-start(bf16[58,512]{1,0:T(8,128)(2,1)S(1)} %get-tuple-element.207), channel_id=1, source_target_pairs={{0,2},{1,3},{2,0},{3,1},{4,6},{5,7},{6,4},{7,5},{8,10},{9,11},{10,... | collective-permute-start | bytes 178184 | tf_op jit(solution)/shard_map/ppermute | solution.py:27
  27.8 1.8 %collective-permute-start.5 = (bf16[58,512]{1,0:T(8,128)(2,1)S(1)}, bf16[58,512]{1,0:T(8,128)(2,1)S(1)}, u32[]{:S(2)}, u32[]{:S(2)}) collective-permute-start(bf16[58,512]{1,0:T(8,128)(2,1)S(1)} %get-tuple-element.205), channel_id=1, source_target_pairs={{0,4},{1,5},{2,6},{3,7},{4,0},{5,1},{6,2},{7,3},{8,12},{9,13},{10,... | collective-permute-start | bytes 178184 | tf_op jit(solution)/shard_map/ppermute | solution.py:27
  29.7 2.7 %collective-permute-start.7 = (bf16[58,512]{1,0:T(8,128)(2,1)S(1)}, bf16[58,512]{1,0:T(8,128)(2,1)S(1)}, u32[]{:S(2)}, u32[]{:S(2)}) collective-permute-start(bf16[58,512]{1,0:T(8,128)(2,1)S(1)} %get-tuple-element.203), channel_id=1, source_target_pairs={{0,6},{1,7},{2,4},{3,5},{4,2},{5,3},{6,0},{7,1},{8,14},{9,15},{10,... | collective-permute-start | bytes 178184 | tf_op jit(solution)/shard_map/ppermute | solution.py:27
  32.5 0.1 collective-permute-start.8
  32.6 2.7 %collective-permute-start.9 = (bf16[58,512]{1,0:T(8,128)(2,1)S(1)}, bf16[58,512]{1,0:T(8,128)(2,1)S(1)}, u32[]{:S(2)}, u32[]{:S(2)}) collective-permute-start(bf16[58,512]{1,0:T(8,128)(2,1)S(1)} %get-tuple-element.201), channel_id=1, source_target_pairs={{0,8},{1,9},{2,10},{3,11},{4,12},{5,13},{6,14},{7,15},{8,0},{9,1},... | collective-permute-start | bytes 178184 | tf_op jit(solution)/shard_map/ppermute | solution.py:27
  35.4 1.0 collective-permute-start.10
  36.3 2.7 %collective-permute-start.11 = (bf16[58,512]{1,0:T(8,128)(2,1)S(1)}, bf16[58,512]{1,0:T(8,128)(2,1)S(1)}, u32[]{:S(2)}, u32[]{:S(2)}) collective-permute-start(bf16[58,512]{1,0:T(8,128)(2,1)S(1)} %get-tuple-element.199), channel_id=1, source_target_pairs={{0,10},{1,11},{2,8},{3,9},{4,14},{5,15},{6,12},{7,13},{8,2},{9,3},... | collective-permute-start | bytes 178184 | tf_op jit(solution)/shard_map/ppermute | solution.py:27
  39.1 0.7 collective-permute-start.12
  39.7 3.1 %collective-permute-start.13 = (bf16[58,512]{1,0:T(8,128)(2,1)S(1)}, bf16[58,512]{1,0:T(8,128)(2,1)S(1)}, u32[]{:S(2)}, u32[]{:S(2)}) collective-permute-start(bf16[58,512]{1,0:T(8,128)(2,1)S(1)} %get-tuple-element.197), channel_id=1, source_target_pairs={{0,12},{1,13},{2,14},{3,15},{4,8},{5,9},{6,10},{7,11},{8,4},{9,5},... | collective-permute-start | bytes 178184 | tf_op jit(solution)/shard_map/ppermute | solution.py:27
  42.9 3.8 %collective-permute-start.14 = (bf16[58,512]{1,0:T(8,128)(2,1)S(1)}, bf16[58,512]{1,0:T(8,128)(2,1)S(1)}, u32[]{:S(2)}, u32[]{:S(2)}) collective-permute-start(bf16[58,512]{1,0:T(8,128)(2,1)S(1)} %get-tuple-element.196), channel_id=1, source_target_pairs={{0,13},{1,12},{2,15},{3,14},{4,9},{5,8},{6,11},{7,10},{8,5},{9,4},... | collective-permute-start | bytes 178184 | tf_op jit(solution)/shard_map/ppermute | solution.py:27
  46.6 0.8 collective-permute-done.10
  47.5 3.3 %collective-permute-start.15 = (bf16[58,512]{1,0:T(8,128)(2,1)S(1)}, bf16[58,512]{1,0:T(8,128)(2,1)S(1)}, u32[]{:S(2)}, u32[]{:S(2)}) collective-permute-start(bf16[58,512]{1,0:T(8,128)(2,1)S(1)} %get-tuple-element.195), channel_id=1, source_target_pairs={{0,14},{1,15},{2,12},{3,13},{4,10},{5,11},{6,8},{7,9},{8,6},{9,7},... | collective-permute-start | bytes 178184 | tf_op jit(solution)/shard_map/ppermute | solution.py:27
  50.8 0.8 collective-permute-done.11
  51.6 2.1 %collective-permute-start.16 = (bf16[58,512]{1,0:T(8,128)(2,1)S(1)}, bf16[58,512]{1,0:T(8,128)(2,1)S(1)}, u32[]{:S(2)}, u32[]{:S(2)}) collective-permute-start(bf16[58,512]{1,0:T(8,128)(2,1)S(1)} %get-tuple-element.194), channel_id=1, source_target_pairs={{0,15},{1,14},{2,13},{3,12},{4,11},{5,10},{6,9},{7,8},{8,7},{9,6},... | collective-permute-start | bytes 178184 | tf_op jit(solution)/shard_map/ppermute | solution.py:27
  53.8 0.8 collective-permute-done.15
  54.6 4.2 %collective-permute-done.16 = bf16[58,512]{1,0:T(8,128)(2,1)S(1)} collective-permute-done((bf16[58,512]{1,0:T(8,128)(2,1)S(1)}, bf16[58,512]{1,0:T(8,128)(2,1)S(1)}, u32[]{:S(2)}, u32[]{:S(2)}) %collective-permute-start.16) | collective-permute-done | bytes 59424 | tf_op jit(solution)/shard_map/ppermute | solution.py:27
  58.8 0.6 gather_fusion.1
  59.4 0.3 reshape.426
  59.7 2.1 %gather_fusion.2 = bf16[384,512]{1,0:T(8,128)(2,1)S(1)} fusion(bf16[928,512]{1,0:T(8,128)(2,1)S(1)} %reshape.426, s32[1024]{0:T(1024)S(1)} %get-tuple-element.221), kind=kCustom, calls=%fused_computation.2 | custom fusion | bytes 787968 | tf_op jit(solution)/shard_map/gather | solution.py:117
  61.8 0.4 fusion.12
  62.2 34.5 %while.18 = (s32[]{:T(128)}, bf16[384,512]{1,0:T(8,128)(2,1)S(1)}, bf16[384,512]{1,0:T(8,128)(2,1)S(1)}, f32[384]{0:T(512)S(1)}, s32[384]{0:T(512)S(1)}, /*index...) while((s32[]{:T(128)}, bf16[384,512]{1,0:T(8,128)(2,1)S(1)}, ...), condition=%wide.region_26.27_spmd.clone, body=%wide.region_21.26_spmd.clone.sunk | while | flops 303321984 | bytes 6322649 | solution.py:138
  62.2 2.0 %collective-permute-start = (bf16[384,512]{1,0:T(8,128)(2,1)S(1)}, bf16[384,512]{1,0:T(8,128)(2,1)S(1)}, u32[]{:S(2)}, u32[]{:S(2)}) collective-permute-start(bf16[384,512]{1,0:T(8,128)(2,1)S(1)} %get-tuple-element.291), channel_id=1, source_target_pairs={{0,1},{1,2},{2,3},{3,4},{4,5},{5,6},{6,7},{7,8},{8,9},{9,10},{10,1... | collective-permute-start | bytes 1179656 | tf_op jit(solution)/shard_map/while/body/eval_jaxpr/ppermute | solution.py:35
  64.2 1.3 collective-permute-start.1
  65.7 2.2 %collective-permute-done.1 = bf16[384,512]{1,0:T(8,128)(2,1)S(1)} collective-permute-done((bf16[384,512]{1,0:T(8,128)(2,1)S(1)}, bf16[384,512]{1,0:T(8,128)(2,1)S(1)}, u32[]{:S(2)}, u32[]{:S(2)}) %collective-permute-start.1) | collective-permute-done | bytes 393248 | tf_op jit(solution)/shard_map/while/body/eval_jaxpr/ppermute | solution.py:35
  67.8 0.4 fusion.90
  68.3 0.4 fusion.91
  68.8 8.0 %collective-permute-start = (bf16[384,512]{1,0:T(8,128)(2,1)S(1)}, bf16[384,512]{1,0:T(8,128)(2,1)S(1)}, u32[]{:S(2)}, u32[]{:S(2)}) collective-permute-start(bf16[384,512]{1,0:T(8,128)(2,1)S(1)} %get-tuple-element.291), channel_id=1, source_target_pairs={{0,1},{1,2},{2,3},{3,4},{4,5},{5,6},{6,7},{7,8},{8,9},{9,10},{10,1... | collective-permute-start | bytes 1179656 | tf_op jit(solution)/shard_map/while/body/eval_jaxpr/ppermute | solution.py:35
  76.7 1.3 collective-permute-start.1
  78.2 2.2 %collective-permute-done.1 = bf16[384,512]{1,0:T(8,128)(2,1)S(1)} collective-permute-done((bf16[384,512]{1,0:T(8,128)(2,1)S(1)}, bf16[384,512]{1,0:T(8,128)(2,1)S(1)}, u32[]{:S(2)}, u32[]{:S(2)}) %collective-permute-start.1) | collective-permute-done | bytes 393248 | tf_op jit(solution)/shard_map/while/body/eval_jaxpr/ppermute | solution.py:35
  80.3 0.4 fusion.90
  80.8 0.4 fusion.91
  81.3 10.9 %collective-permute-start = (bf16[384,512]{1,0:T(8,128)(2,1)S(1)}, bf16[384,512]{1,0:T(8,128)(2,1)S(1)}, u32[]{:S(2)}, u32[]{:S(2)}) collective-permute-start(bf16[384,512]{1,0:T(8,128)(2,1)S(1)} %get-tuple-element.291), channel_id=1, source_target_pairs={{0,1},{1,2},{2,3},{3,4},{4,5},{5,6},{6,7},{7,8},{8,9},{9,10},{10,1... | collective-permute-start | bytes 1179656 | tf_op jit(solution)/shard_map/while/body/eval_jaxpr/ppermute | solution.py:35
  92.2 1.3 collective-permute-start.1
  93.7 2.2 %collective-permute-done.1 = bf16[384,512]{1,0:T(8,128)(2,1)S(1)} collective-permute-done((bf16[384,512]{1,0:T(8,128)(2,1)S(1)}, bf16[384,512]{1,0:T(8,128)(2,1)S(1)}, u32[]{:S(2)}, u32[]{:S(2)}) %collective-permute-start.1) | collective-permute-done | bytes 393248 | tf_op jit(solution)/shard_map/while/body/eval_jaxpr/ppermute | solution.py:35
  95.8 0.4 fusion.90
  96.3 0.4 fusion.91
  96.8 2.9 %scatter_custom_fusion.2 = f32[928]{0:T(1024)S(1)} fusion(s32[384]{0:T(512)S(1)} %fusion.58, f32[384]{0:T(512)S(1)} %get-tuple-element.141, f32[]{:T(128)} %constant.155.clone.1), kind=kCustom, calls=%fused_computation.163 | custom fusion | bytes 3716 | tf_op jit(solution)/shard_map/scatter | solution.py:141
  99.7 0.7 all_to_all.8
  100.4 13.4 %all-to-all-start = ((f32[16,58,1]{1,2,0:T(1,128)}), f32[16,58,1]{1,2,0:T(1,128)S(1)}, u32[]{:S(2)}, u32[]{:S(2)}) async-start(f32[16,58,1]{1,2,0:T(1,128)} %bitcast.40), calls=%async_computation | async-start | bytes 16384 | tf_op jit(solution)/shard_map/all_to_all | solution.py:143
  113.8 1.4 %fusion.13 = f32[384]{0:T(512)S(1)} fusion(bf16[384,512]{1,0:T(8,128)(2,1)S(1)} %fusion.15, f32[64,512]{1,0:T(8,128)} %all-reduce.2.cloned.1.call-done, s32[384]{0:T(512)S(1)} %copy-done.1), kind=kOutput, calls=%fused_computation.29 | convolution fusion | flops 151068288 | bytes 527360 | tf_op jit(solution)/shard_map/dot_general | solution.py:158
  115.2 5.0 %all-to-all-done = f32[16,58,1]{1,2,0:T(1,128)S(1)} async-done(((f32[16,58,1]{1,2,0:T(1,128)}), f32[16,58,1]{1,2,0:T(1,128)S(1)}, u32[]{:S(2)}, u32[]{:S(2)}) %all-to-all-start) | async-done | bytes 3744 | tf_op jit(solution)/shard_map/all_to_all | solution.py:143
  120.2 0.5 broadcast.584
  120.7 0.7 reduce.13
  121.5 1.9 %gather_fusion.3 = f32[384]{0:T(512)S(1)} fusion(f32[928]{0:T(1024)S(1)} %all_to_all.10, s32[1024]{0:T(1024)S(1)} %pad_clamp_fusion), kind=kCustom, calls=%fused_computation.3 | custom fusion | bytes 4608 | tf_op jit(solution)/shard_map/gather | solution.py:144
  123.4 0.6 convert_divide_fusion
  (93 shorter events, 2.2 us)
Async XLA Ops:
  7.2 1.3 copy-start
  7.2 106.6 %all-reduce.2.cloned.1.call-start = ((), (), s32[]{:S(2)}) async-start(), calls=%async_computation.1 | async-start | bytes 262144 | tf_op jit(solution)/shard_map/psum | solution.py:154
  8.4 0.7 copy-start.1
  10.0 0.7 copy-start.2
  24.6 5.1 %collective-permute-start.2 = (bf16[58,512]{1,0:T(8,128)(2,1)S(1)}, bf16[58,512]{1,0:T(8,128)(2,1)S(1)}, u32[]{:S(2)}, u32[]{:S(2)}) collective-permute-start(bf16[58,512]{1,0:T(8,128)(2,1)S(1)} %get-tuple-element.208), channel_id=1, source_target_pairs={{0,1},{1,0},{2,3},{3,2},{4,5},{5,4},{6,7},{7,6},{8,9},{9,8},{10,11... | collective-permute-start | bytes 178184 | tf_op jit(solution)/shard_map/ppermute | solution.py:27
  25.2 7.3 %collective-permute-start.3 = (bf16[58,512]{1,0:T(8,128)(2,1)S(1)}, bf16[58,512]{1,0:T(8,128)(2,1)S(1)}, u32[]{:S(2)}, u32[]{:S(2)}) collective-permute-start(bf16[58,512]{1,0:T(8,128)(2,1)S(1)} %get-tuple-element.207), channel_id=1, source_target_pairs={{0,2},{1,3},{2,0},{3,1},{4,6},{5,7},{6,4},{7,5},{8,10},{9,11},{10,... | collective-permute-start | bytes 178184 | tf_op jit(solution)/shard_map/ppermute | solution.py:27
  27.8 4.8 %collective-permute-start.4 = (bf16[58,512]{1,0:T(8,128)(2,1)S(1)}, bf16[58,512]{1,0:T(8,128)(2,1)S(1)}, u32[]{:S(2)}, u32[]{:S(2)}) collective-permute-start(bf16[58,512]{1,0:T(8,128)(2,1)S(1)} %get-tuple-element.206), channel_id=1, source_target_pairs={{0,3},{1,2},{2,1},{3,0},{4,7},{5,6},{6,5},{7,4},{8,11},{9,10},{10,... | collective-permute-start | bytes 178184 | tf_op jit(solution)/shard_map/ppermute | solution.py:27
  27.8 7.5 %collective-permute-start.5 = (bf16[58,512]{1,0:T(8,128)(2,1)S(1)}, bf16[58,512]{1,0:T(8,128)(2,1)S(1)}, u32[]{:S(2)}, u32[]{:S(2)}) collective-permute-start(bf16[58,512]{1,0:T(8,128)(2,1)S(1)} %get-tuple-element.205), channel_id=1, source_target_pairs={{0,4},{1,5},{2,6},{3,7},{4,0},{5,1},{6,2},{7,3},{8,12},{9,13},{10,... | collective-permute-start | bytes 178184 | tf_op jit(solution)/shard_map/ppermute | solution.py:27
  29.6 6.7 %collective-permute-start.6 = (bf16[58,512]{1,0:T(8,128)(2,1)S(1)}, bf16[58,512]{1,0:T(8,128)(2,1)S(1)}, u32[]{:S(2)}, u32[]{:S(2)}) collective-permute-start(bf16[58,512]{1,0:T(8,128)(2,1)S(1)} %get-tuple-element.204), channel_id=1, source_target_pairs={{0,5},{1,4},{2,7},{3,6},{4,1},{5,0},{6,3},{7,2},{8,13},{9,12},{10,... | collective-permute-start | bytes 178184 | tf_op jit(solution)/shard_map/ppermute | solution.py:27
  29.7 9.3 %collective-permute-start.7 = (bf16[58,512]{1,0:T(8,128)(2,1)S(1)}, bf16[58,512]{1,0:T(8,128)(2,1)S(1)}, u32[]{:S(2)}, u32[]{:S(2)}) collective-permute-start(bf16[58,512]{1,0:T(8,128)(2,1)S(1)} %get-tuple-element.203), channel_id=1, source_target_pairs={{0,6},{1,7},{2,4},{3,5},{4,2},{5,3},{6,0},{7,1},{8,14},{9,15},{10,... | collective-permute-start | bytes 178184 | tf_op jit(solution)/shard_map/ppermute | solution.py:27
  32.5 7.3 %collective-permute-start.8 = (bf16[58,512]{1,0:T(8,128)(2,1)S(1)}, bf16[58,512]{1,0:T(8,128)(2,1)S(1)}, u32[]{:S(2)}, u32[]{:S(2)}) collective-permute-start(bf16[58,512]{1,0:T(8,128)(2,1)S(1)} %get-tuple-element.202), channel_id=1, source_target_pairs={{0,7},{1,6},{2,5},{3,4},{4,3},{5,2},{6,1},{7,0},{8,15},{9,14},{10,... | collective-permute-start | bytes 178184 | tf_op jit(solution)/shard_map/ppermute | solution.py:27
  32.6 10.3 %collective-permute-start.9 = (bf16[58,512]{1,0:T(8,128)(2,1)S(1)}, bf16[58,512]{1,0:T(8,128)(2,1)S(1)}, u32[]{:S(2)}, u32[]{:S(2)}) collective-permute-start(bf16[58,512]{1,0:T(8,128)(2,1)S(1)} %get-tuple-element.201), channel_id=1, source_target_pairs={{0,8},{1,9},{2,10},{3,11},{4,12},{5,13},{6,14},{7,15},{8,0},{9,1},... | collective-permute-start | bytes 178184 | tf_op jit(solution)/shard_map/ppermute | solution.py:27
  35.4 12.1 %collective-permute-start.10 = (bf16[58,512]{1,0:T(8,128)(2,1)S(1)}, bf16[58,512]{1,0:T(8,128)(2,1)S(1)}, u32[]{:S(2)}, u32[]{:S(2)}) collective-permute-start(bf16[58,512]{1,0:T(8,128)(2,1)S(1)} %get-tuple-element.200), channel_id=1, source_target_pairs={{0,9},{1,8},{2,11},{3,10},{4,13},{5,12},{6,15},{7,14},{8,1},{9,0},... | collective-permute-start | bytes 178184 | tf_op jit(solution)/shard_map/ppermute | solution.py:27
  36.3 15.3 %collective-permute-start.11 = (bf16[58,512]{1,0:T(8,128)(2,1)S(1)}, bf16[58,512]{1,0:T(8,128)(2,1)S(1)}, u32[]{:S(2)}, u32[]{:S(2)}) collective-permute-start(bf16[58,512]{1,0:T(8,128)(2,1)S(1)} %get-tuple-element.199), channel_id=1, source_target_pairs={{0,10},{1,11},{2,8},{3,9},{4,14},{5,15},{6,12},{7,13},{8,2},{9,3},... | collective-permute-start | bytes 178184 | tf_op jit(solution)/shard_map/ppermute | solution.py:27
  39.1 14.6 %collective-permute-start.12 = (bf16[58,512]{1,0:T(8,128)(2,1)S(1)}, bf16[58,512]{1,0:T(8,128)(2,1)S(1)}, u32[]{:S(2)}, u32[]{:S(2)}) collective-permute-start(bf16[58,512]{1,0:T(8,128)(2,1)S(1)} %get-tuple-element.198), channel_id=1, source_target_pairs={{0,11},{1,10},{2,9},{3,8},{4,15},{5,14},{6,13},{7,12},{8,3},{9,2},... | collective-permute-start | bytes 178184 | tf_op jit(solution)/shard_map/ppermute | solution.py:27
  39.7 14.0 %collective-permute-start.13 = (bf16[58,512]{1,0:T(8,128)(2,1)S(1)}, bf16[58,512]{1,0:T(8,128)(2,1)S(1)}, u32[]{:S(2)}, u32[]{:S(2)}) collective-permute-start(bf16[58,512]{1,0:T(8,128)(2,1)S(1)} %get-tuple-element.197), channel_id=1, source_target_pairs={{0,12},{1,13},{2,14},{3,15},{4,8},{5,9},{6,10},{7,11},{8,4},{9,5},... | collective-permute-start | bytes 178184 | tf_op jit(solution)/shard_map/ppermute | solution.py:27
  42.9 10.9 %collective-permute-start.14 = (bf16[58,512]{1,0:T(8,128)(2,1)S(1)}, bf16[58,512]{1,0:T(8,128)(2,1)S(1)}, u32[]{:S(2)}, u32[]{:S(2)}) collective-permute-start(bf16[58,512]{1,0:T(8,128)(2,1)S(1)} %get-tuple-element.196), channel_id=1, source_target_pairs={{0,13},{1,12},{2,15},{3,14},{4,9},{5,8},{6,11},{7,10},{8,5},{9,4},... | collective-permute-start | bytes 178184 | tf_op jit(solution)/shard_map/ppermute | solution.py:27
  47.5 7.1 %collective-permute-start.15 = (bf16[58,512]{1,0:T(8,128)(2,1)S(1)}, bf16[58,512]{1,0:T(8,128)(2,1)S(1)}, u32[]{:S(2)}, u32[]{:S(2)}) collective-permute-start(bf16[58,512]{1,0:T(8,128)(2,1)S(1)} %get-tuple-element.195), channel_id=1, source_target_pairs={{0,14},{1,15},{2,12},{3,13},{4,10},{5,11},{6,8},{7,9},{8,6},{9,7},... | collective-permute-start | bytes 178184 | tf_op jit(solution)/shard_map/ppermute | solution.py:27
  51.6 7.2 %collective-permute-start.16 = (bf16[58,512]{1,0:T(8,128)(2,1)S(1)}, bf16[58,512]{1,0:T(8,128)(2,1)S(1)}, u32[]{:S(2)}, u32[]{:S(2)}) collective-permute-start(bf16[58,512]{1,0:T(8,128)(2,1)S(1)} %get-tuple-element.194), channel_id=1, source_target_pairs={{0,15},{1,14},{2,13},{3,12},{4,11},{5,10},{6,9},{7,8},{8,7},{9,6},... | collective-permute-start | bytes 178184 | tf_op jit(solution)/shard_map/ppermute | solution.py:27
  62.2 6.0 %collective-permute-start = (bf16[384,512]{1,0:T(8,128)(2,1)S(1)}, bf16[384,512]{1,0:T(8,128)(2,1)S(1)}, u32[]{:S(2)}, u32[]{:S(2)}) collective-permute-start(bf16[384,512]{1,0:T(8,128)(2,1)S(1)} %get-tuple-element.291), channel_id=1, source_target_pairs={{0,1},{1,2},{2,3},{3,4},{4,5},{5,6},{6,7},{7,8},{8,9},{9,10},{10,1... | collective-permute-start | bytes 1179656 | tf_op jit(solution)/shard_map/while/body/eval_jaxpr/ppermute | solution.py:35
  64.2 3.6 %collective-permute-start.1 = (bf16[384,512]{1,0:T(8,128)(2,1)S(1)}, bf16[384,512]{1,0:T(8,128)(2,1)S(1)}, u32[]{:S(2)}, u32[]{:S(2)}) collective-permute-start(bf16[384,512]{1,0:T(8,128)(2,1)S(1)} %get-tuple-element.292), channel_id=1, source_target_pairs={{1,0},{2,1},{3,2},{4,3},{5,4},{6,5},{7,6},{8,7},{9,8},{10,9},{11,1... | collective-permute-start | bytes 1179656 | tf_op jit(solution)/shard_map/while/body/eval_jaxpr/ppermute | solution.py:35
  68.8 12.0 %collective-permute-start = (bf16[384,512]{1,0:T(8,128)(2,1)S(1)}, bf16[384,512]{1,0:T(8,128)(2,1)S(1)}, u32[]{:S(2)}, u32[]{:S(2)}) collective-permute-start(bf16[384,512]{1,0:T(8,128)(2,1)S(1)} %get-tuple-element.291), channel_id=1, source_target_pairs={{0,1},{1,2},{2,3},{3,4},{4,5},{5,6},{6,7},{7,8},{8,9},{9,10},{10,1... | collective-permute-start | bytes 1179656 | tf_op jit(solution)/shard_map/while/body/eval_jaxpr/ppermute | solution.py:35
  76.7 3.6 %collective-permute-start.1 = (bf16[384,512]{1,0:T(8,128)(2,1)S(1)}, bf16[384,512]{1,0:T(8,128)(2,1)S(1)}, u32[]{:S(2)}, u32[]{:S(2)}) collective-permute-start(bf16[384,512]{1,0:T(8,128)(2,1)S(1)} %get-tuple-element.292), channel_id=1, source_target_pairs={{1,0},{2,1},{3,2},{4,3},{5,4},{6,5},{7,6},{8,7},{9,8},{10,9},{11,1... | collective-permute-start | bytes 1179656 | tf_op jit(solution)/shard_map/while/body/eval_jaxpr/ppermute | solution.py:35
  81.3 15.0 %collective-permute-start = (bf16[384,512]{1,0:T(8,128)(2,1)S(1)}, bf16[384,512]{1,0:T(8,128)(2,1)S(1)}, u32[]{:S(2)}, u32[]{:S(2)}) collective-permute-start(bf16[384,512]{1,0:T(8,128)(2,1)S(1)} %get-tuple-element.291), channel_id=1, source_target_pairs={{0,1},{1,2},{2,3},{3,4},{4,5},{5,6},{6,7},{7,8},{8,9},{9,10},{10,1... | collective-permute-start | bytes 1179656 | tf_op jit(solution)/shard_map/while/body/eval_jaxpr/ppermute | solution.py:35
  92.2 3.6 %collective-permute-start.1 = (bf16[384,512]{1,0:T(8,128)(2,1)S(1)}, bf16[384,512]{1,0:T(8,128)(2,1)S(1)}, u32[]{:S(2)}, u32[]{:S(2)}) collective-permute-start(bf16[384,512]{1,0:T(8,128)(2,1)S(1)} %get-tuple-element.292), channel_id=1, source_target_pairs={{1,0},{2,1},{3,2},{4,3},{5,4},{6,5},{7,6},{8,7},{9,8},{10,9},{11,1... | collective-permute-start | bytes 1179656 | tf_op jit(solution)/shard_map/while/body/eval_jaxpr/ppermute | solution.py:35
  100.4 19.8 %all-to-all-start = ((f32[16,58,1]{1,2,0:T(1,128)}), f32[16,58,1]{1,2,0:T(1,128)S(1)}, u32[]{:S(2)}, u32[]{:S(2)}) async-start(f32[16,58,1]{1,2,0:T(1,128)} %bitcast.40), calls=%async_computation | async-start | bytes 16384 | tf_op jit(solution)/shard_map/all_to_all | solution.py:143
Sparse Core Ops, SparseCore 0:
  11.4 97.3 all-reduce.1
